TPU v7x, 128 devices: a whole 4x4x4 slice. The times are simulated.
128 devices in a mesh: dp: 16 (over y_hi, x, core), mp: 8 (over z, y_lo).
Axes of the slice: x: 4, y: 4 (y_hi: 2, y_lo: 2; y = y_hi * 2 + y_lo), z: 4, core: 2. Of those that a mesh axis runs over, the one named last changes fastest.
Arguments:
- hidden_states: bfloat16 [65536, 4096], P('dp', 'mp'), may hold values from -1 to 1
- factor_values: bfloat16 [65536, 128], P('dp', 'mp'), may hold values from 0.029907227 to 0.13964844
- class_ids: int32 [65536, 128], P('dp', 'mp'), may hold values from 0 to 128255, as said below
- centers: int32 [3], replicated, may hold values from 0 to 65535
Outputs:
- min_distance: float32 [65536], P(('dp', 'mp'))
- weight_means: float32 [3], replicated
Inputs may be any that keep to these rules, and one draw needn't show every extreme that they name: `centers`: each value is a sample index. `class_ids`: entries k * 16 to (k + 1) * 16 - 1 of a row hold distinct classes of the k-th of 8 equal ranges of the vocabulary.
All inputs are finite; a program needn't handle non-finite values.
Results may differ from a plain program's by a relative error of at most 0.00095.
Values may be sent and summed in bfloat16 or wider, within the bound.
No kernel may reach another device: no remote copies, remote signals or barrier semaphores. Data moves between devices by JAX's collectives and lax.ppermute only.
A program may use at most 64 MiB of HBM per device.

v0:
```python
import functools

import jax
import jax.numpy as jnp
from jax import lax
from jax.sharding import Mesh
from jax.sharding import PartitionSpec as P

K_LOC = 16
STEPS = 3
MP = ("mp_0", "mp_1")
DP = ("dp_0", "dp_1", "dp_2")
DP_MP = ("dp_0", "dp_1", "dp_2", "mp_0", "mp_1")


def split_up(shard, dim, length):
    before, after = (shard.shape[:dim], shard.shape[dim + 1 :])
    return jnp.moveaxis(shard.reshape(*before, length, -1, *after), dim, 0)


def summed_on_arrival(shard, axis, dim):
    length = lax.axis_size(axis)
    parts = lax.all_to_all(split_up(shard, dim, length), axis, 0, 0, tiled=True)
    return jnp.sum(parts, axis=0)


def by_axis(shard, axes):
    return functools.reduce(lax.psum, axes, shard)


def match_sum(idents, values, id_row, val_row):
    nblk = idents.shape[1] // K_LOC
    match = idents.reshape(-1, nblk, K_LOC, 1) == id_row.reshape(1, nblk, 1, K_LOC)
    prod = values.astype(jnp.float32).reshape(-1, nblk, K_LOC, 1) * val_row.astype(
        jnp.float32
    ).reshape(1, nblk, 1, K_LOC)
    return jnp.sum(jnp.where(match, prod, jnp.float32(0.0)), axis=(1, 2, 3))


def squares(values):
    return jnp.sum(jnp.square(values.astype(jnp.float32)), axis=1)


def body(hidden_states, factor_values, class_ids, centers):
    partial_sums = []
    min_distance = None
    rows_all = hidden_states.shape[0]
    rows = rows_all // lax.axis_size(MP)
    device_pos = lax.axis_index(DP)
    model_pos = lax.axis_index(MP)
    width_h = hidden_states.shape[1]
    width_a = factor_values.shape[1]
    start_h = model_pos * width_h
    start_a = model_pos * width_a
    full_h = width_h * lax.axis_size(MP)
    full_a = width_a * lax.axis_size(MP)
    owners = centers // rows_all
    offsets = centers - owners * rows_all
    mine = (owners == device_pos).astype(jnp.float32)[:, None]
    pick_h = hidden_states[offsets].astype(jnp.float32) * mine
    pick_v = factor_values[offsets].astype(jnp.float32) * mine
    pick_i = class_ids[offsets].astype(jnp.float32) * mine
    count = centers.shape[0]
    table_h = lax.dynamic_update_slice(
        jnp.zeros((count, full_h), jnp.float32), pick_h, (0, start_h)
    )
    table_v = lax.dynamic_update_slice(
        jnp.zeros((count, full_a), jnp.float32), pick_v, (0, start_a)
    )
    table_i = lax.dynamic_update_slice(
        jnp.zeros((count, full_a), jnp.float32), pick_i, (0, start_a)
    )
    table_h, table_v, table_i = lax.psum((table_h, table_v, table_i), DP_MP)
    center_hn = jnp.sum(table_h * table_h, axis=1)
    center_an = jnp.sum(table_v * table_v, axis=1)
    local_h = lax.dynamic_slice_in_dim(table_h, start_h, width_h, 1).astype(jnp.bfloat16)
    local_v = lax.dynamic_slice_in_dim(table_v, start_a, width_a, 1).astype(jnp.bfloat16)
    local_i = lax.dynamic_slice_in_dim(table_i, start_a, width_a, 1).astype(jnp.int32)
    prods_h = jnp.dot(hidden_states, local_h.T, preferred_element_type=jnp.float32)
    prods_a = [
        match_sum(class_ids, factor_values, local_i[step], local_v[step]) for step in range(STEPS)
    ]
    pieces = [squares(hidden_states), squares(factor_values)]
    pieces = pieces + [prods_h[:, step] for step in range(STEPS)] + prods_a
    summed = summed_on_arrival(jnp.stack(pieces), MP, 1)
    sq_h = summed[0]
    sq_a = summed[1]
    pool_total = rows * lax.axis_size(DP) * lax.axis_size(MP)
    for step in range(STEPS):
        inner_h = summed[2 + step]
        inner_a = summed[2 + STEPS + step]
        norm_hc = center_hn[step]
        norm_ac = center_an[step]
        dist = jnp.maximum(
            sq_h * sq_a + norm_hc * norm_ac - 2.0 * inner_h * inner_a, jnp.float32(0.0)
        )
        min_distance = dist if step == 0 else jnp.minimum(min_distance, dist)
        partial_sums.append(jnp.sum(min_distance))
    weight_means = by_axis(jnp.stack(partial_sums), DP_MP) / pool_total
    return (min_distance, weight_means)


def solution(mesh):
    finer = Mesh(mesh.devices.reshape(2, 4, 2, 4, 2), ("dp_0", "dp_1", "dp_2", "mp_0", "mp_1"))
    return jax.shard_map(
        body,
        mesh=finer,
        in_specs=(P(DP, MP), P(DP, MP), P(DP, MP), P()),
        out_specs=(P(DP_MP), P()),
        check_vma=False,
    )
```

profile of v0, /device:TPU:0, one launch (start us, length us, event | category | flops | bytes accessed | tf_op | source)
XLA Modules:
  0.0 137.4 jit_solution(7775207025141159430)
XLA Ops:
  0.6 1.4 %copy.18 = bf16[4096,16]{1,0:T(8,128)(2,1)S(1)} copy(bf16[4096,16]{0,1:T(8,128)(2,1)} %param.5) | data formatting | bytes 262144 | tf_op args[1]
  2.0 1.6 %convert_element_type.61 = f32[4096,16]{0,1:T(8,128)} convert(bf16[4096,16]{0,1:T(8,128)(2,1)} %param.5) | non-fusion elementwise | flops 65536 | bytes 393216 | tf_op jit(solution)/shard_map/convert_element_type | solution.py:41
  3.6 1.0 multiply_reduce_fusion.1
  4.6 0.7 compare_convert_fusion
  5.3 0.7 compare_select_fusion
  5.9 1.5 %copy.17 = s32[4096,16]{1,0:T(8,128)S(1)} copy(s32[4096,16]{0,1:T(8,128)} %param.6) | data formatting | bytes 524288 | tf_op args[2]
  7.5 3.1 %multiply_reduce_fusion = f32[4096]{0:T(1024)S(1)} fusion(bf16[4096,512]{1,0:T(8,128)(2,1)} %param.4), kind=kLoop, calls=%fused_computation.3 | loop fusion | flops 6287360 | bytes 4210688 | tf_op jit(solution)/shard_map/reduce_sum | solution.py:41
  10.6 3.3 %gather_fusion = bf16[3,512]{1,0:T(4,128)(2,1)S(1)} fusion(bf16[4096,512]{1,0:T(8,128)(2,1)} %param.4, s32[1024]{0:T(1024)S(1)} %pad_clamp_fusion), kind=kCustom, calls=%fused_computation | custom fusion | bytes 6156 | tf_op jit(solution)/shard_map/gather | solution.py:60
  15.5 68.8 %all-reduce = (f32[3,4096]{1,0:T(4,128)S(1)}, f32[3,128]{1,0:T(4,128)S(1)}, f32[3,128]{1,0:T(4,128)S(1)}) all-reduce(f32[3,4096]{1,0:T(4,128)S(1)} %multiply_dynamic-update-slice_fusion, f32[3,128]{1,0:T(4,128)S(1)} %dynamic_update_slice.11, ...), channel_id=1, replica_groups=mesh['dp_0'=2,'dp_1'=4,'dp_2'=2,'mp_0'=4,'mp_1'=2] {'dp_0','dp_1','dp_2'..., use_global_device_ids=true, to_apply=%region_2.3 | all-reduce | flops 13056 | bytes 104448 | tf_op jit(solution)/shard_map/psum | solution.py:73
  84.5 3.4 %convolution_bitcast_fusion = f32[4096,3]{0,1:T(4,128)S(1)} fusion(bf16[4096,512]{1,0:T(8,128)(2,1)} %param.4, f32[3,4096]{1,0:T(4,128)S(1)} %get-tuple-element.5, s32[]{:T(128)S(6)} %select_n.56), kind=kOutput, calls=%fused_computation.4 | convolution fusion | flops 12582912 | bytes 4247556 | tf_op jit(solution)/shard_map/dot_general | solution.py:79
  87.9 2.0 %select_reduce_fusion = (f32[4096]{0:T(1024)S(1)}, f32[4096]{0:T(1024)S(1)}, f32[4096]{0:T(1024)S(1)}) fusion(f32[16]{0:T(128)S(1)} %get-tuple-element.24, f32[4096,16]{0,1:T(8,128)S(1)} %copy-done.1, s32[4096,16]{0,1:T(8,128)S(1)} %copy-done, s32[16]{0:T(128)S(1)} %get-tuple-element.21, f32[16]{0:T(128)S(1)} %get-tuple-element.25, ...), kind=kLoop, calls=%fused_computation.5 | loop fusion | flops 12570624 | bytes 573824 | tf_op jit(solution)/shard_map/reduce_sum | solution.py:37
  89.9 0.8 stack.44
  90.7 3.4 %all-to-all-start = ((f32[8,8,512]{2,1,0:T(8,128)}), f32[8,8,512]{2,1,0:T(8,128)S(1)}, u32[]{:S(2)}, u32[]{:S(2)}) async-start(f32[8,8,512]{2,1,0:T(8,128)} %bitcast.15), calls=%async_computation | async-start | bytes 262144 | tf_op jit(solution)/shard_map/all_to_all | solution.py:23
  94.3 0.7 fusion.10
  98.9 1.8 %all-to-all-done = f32[8,8,512]{2,1,0:T(8,128)S(1)} async-done(((f32[8,8,512]{2,1,0:T(8,128)}), f32[8,8,512]{2,1,0:T(8,128)S(1)}, u32[]{:S(2)}, u32[]{:S(2)}) %all-to-all-start) | async-done | bytes 131104 | tf_op jit(solution)/shard_map/all_to_all | solution.py:23
  100.7 0.7 fusion.5
  101.4 0.6 fusion.7
  102.0 1.2 fusion.8
  103.2 2.0 %pad_maximum_fusion = f32[3]{0:T(128)S(1)} fusion(f32[1]{0:T(128)} %bitcast.22, f32[1]{0:T(128)} %bitcast.21, f32[1]{0:T(128)} %bitcast.20), kind=kLoop, calls=%fused_computation.38 | loop fusion | flops 6 | bytes 24 | tf_op jit(solution)/shard_map/stack | solution.py:99
  105.2 6.4 %psum.59 = f32[3]{0:T(128)S(1)} all-reduce(f32[3]{0:T(128)S(1)} %pad_maximum_fusion), channel_id=1, replica_groups=mesh['dp_0'=2,'dp_1'=4,'dp_2'=2,'mp_0'=4,'mp_1'=2] {'dp_0'}, use_global_device_ids=true, to_apply=%region_14.15 | all-reduce | flops 3 | bytes 24 | tf_op jit(solution)/shard_map/psum | solution.py:28
  111.6 8.9 %psum.60 = f32[3]{0:T(128)S(1)} all-reduce(f32[3]{0:T(128)S(1)} %psum.59), channel_id=1, replica_groups=mesh['dp_0'=2,'dp_1'=4,'dp_2'=2,'mp_0'=4,'mp_1'=2] {'dp_1'}, use_global_device_ids=true, to_apply=%region_15.16 | all-reduce | flops 3 | bytes 24 | tf_op jit(solution)/shard_map/psum | solution.py:28
  120.5 2.5 %psum.61 = f32[3]{0:T(128)S(1)} all-reduce(f32[3]{0:T(128)S(1)} %psum.60), channel_id=1, replica_groups=mesh['dp_0'=2,'dp_1'=4,'dp_2'=2,'mp_0'=4,'mp_1'=2] {'dp_2'}, use_global_device_ids=true, to_apply=%region_16.17 | all-reduce | flops 3 | bytes 24 | tf_op jit(solution)/shard_map/psum | solution.py:28
  123.0 9.0 %psum.62 = f32[3]{0:T(128)S(1)} all-reduce(f32[3]{0:T(128)S(1)} %psum.61), channel_id=1, replica_groups=mesh['dp_0'=2,'dp_1'=4,'dp_2'=2,'mp_0'=4,'mp_1'=2] {'mp_0'}, use_global_device_ids=true, to_apply=%region_17.18 | all-reduce | flops 3 | bytes 24 | tf_op jit(solution)/shard_map/psum | solution.py:28
  132.0 4.9 %psum.63 = f32[3]{0:T(128)S(1)} all-reduce(f32[3]{0:T(128)S(1)} %psum.62), channel_id=1, replica_groups=mesh['dp_0'=2,'dp_1'=4,'dp_2'=2,'mp_0'=4,'mp_1'=2] {'mp_1'}, use_global_device_ids=true, to_apply=%region_18.19 | all-reduce | flops 3 | bytes 24 | tf_op jit(solution)/shard_map/psum | solution.py:28
  (23 shorter events, 2.6 us)
Async XLA Ops:
  7.5 80.4 %copy-start = (s32[4096,16]{0,1:T(8,128)S(1)}, s32[4096,16]{0,1:T(8,128)}, u32[]{:S(2)}) copy-start(s32[4096,16]{0,1:T(8,128)} %param.6) | copy-start | bytes 786436
  14.5 73.4 %copy-start.1 = (f32[4096,16]{0,1:T(8,128)S(1)}, f32[4096,16]{0,1:T(8,128)}, u32[]{:S(2)}) copy-start(f32[4096,16]{0,1:T(8,128)} %convert_element_type.61) | copy-start | bytes 786436
  90.7 10.0 %all-to-all-start = ((f32[8,8,512]{2,1,0:T(8,128)}), f32[8,8,512]{2,1,0:T(8,128)S(1)}, u32[]{:S(2)}, u32[]{:S(2)}) async-start(f32[8,8,512]{2,1,0:T(8,128)} %bitcast.15), calls=%async_computation | async-start | bytes 262144 | tf_op jit(solution)/shard_map/all_to_all | solution.py:23
where the time goes:
time: 138 us; the launch traced here: 137 us
  blocking collectives  101 us (73%)
  other arithmetic  14.5 us (11%)
  local copies, waits for them, and re-layouts  9.23 us (7%)
  between operations  4.63 us (3%)
  starting transfers between devices  3.37 us (2%)
  matrix products  3.36 us (2%)
  waiting for transfers between devices  1.83 us (1%)
    psum x1, blocking collectives, body(): table_h, table_v, table_i = lax.psum((table_h, table_v, table_i), DP_MP)  68.8 us
    psum x5, blocking collectives, by_axis(): return functools.reduce(lax.psum, axes, shard)  31.8 us
    reduce_sum x2, other arithmetic, squares(): return jnp.sum(jnp.square(values.astype(jnp.float32)), axis=1)  4.08 us
    all_to_all x1, starting transfers between devices, summed_on_arrival(): parts = lax.all_to_all(split_up(shard, dim, length), axis, 0, 0, tiled=True)  3.37 us
    dot_general x1, matrix products, body(): jnp.dot(hidden_states, local_h.T, preferred_element_type=jnp.float32)  3.36 us
    gather x1, local copies, waits for them, and re-layouts, body(): pick_h = hidden_states[offsets].astype(jnp.float32) * mine  3.29 us
    unnamed x6, local copies, waits for them, and re-layouts  2.94 us
  transfers between devices with their start and end apart: 1, of which 1 were waited for; matrix products, arithmetic and copies ran while one was open for 1% of the time, Pallas kernels for 0%

commit v1 on v0

v1 whole, which is shorter than its diff:
```python
import functools

import jax
import jax.numpy as jnp
from jax import lax
from jax.experimental import pallas as pl
from jax.experimental.pallas import tpu as pltpu
from jax.sharding import Mesh
from jax.sharding import PartitionSpec as P

K_LOC = 16
STEPS = 3
LANES = 128
MP = ("mp_0", "mp_1")
DP = ("dp_0", "dp_1", "dp_2")
DP_MP = ("dp_0", "dp_1", "dp_2", "mp_0", "mp_1")
VMEM = pltpu.VMEM
F32 = jnp.float32
BF16 = jnp.bfloat16


def vspec():
    return pl.BlockSpec(memory_space=VMEM)


def params(mib):
    return pltpu.CompilerParams(vmem_limit_bytes=mib * 1024 * 1024)


def pick_kernel(centers, hid, val, ids, out, hbuf, vbuf, ibuf, rows, sem):
    rows_all = hid.shape[0]
    copies = []
    for t in range(STEPS):
        off = lax.rem(centers[t], rows_all)
        row8 = pl.multiple_of((off // 8) * 8, 8)
        col = pl.multiple_of((off // LANES) * LANES, LANES)
        copies.append(pltpu.make_async_copy(hid.at[pl.ds(row8, 8), :], hbuf.at[t], sem.at[t, 0]))
        copies.append(pltpu.make_async_copy(val.at[:, pl.ds(col, LANES)], vbuf.at[t], sem.at[t, 1]))
        copies.append(pltpu.make_async_copy(ids.at[:, pl.ds(col, LANES)], ibuf.at[t], sem.at[t, 2]))
    for c in copies:
        c.start()
    chunks = hid.shape[1] // LANES
    rows[...] = jnp.zeros_like(rows)
    lane = lax.broadcasted_iota(jnp.int32, (K_LOC, LANES), 1)
    cols = jnp.zeros((K_LOC, LANES), F32)
    for c in copies:
        c.wait()
    for t in range(STEPS):
        off = lax.rem(centers[t], rows_all)
        blk = hbuf[t].astype(F32)
        here = lax.broadcasted_iota(jnp.int32, blk.shape, 0) == lax.rem(off, 8)
        row = jnp.sum(jnp.where(here, blk, 0.0), axis=0, keepdims=True)
        for j in range(chunks):
            rows[t * chunks + j : t * chunks + j + 1, :] = row[:, j * LANES : (j + 1) * LANES]
        here = lane == lax.rem(off, LANES)
        vcol = jnp.sum(jnp.where(here, vbuf[t].astype(F32), 0.0), axis=1, keepdims=True)
        icol = jnp.sum(jnp.where(here, ibuf[t], 0), axis=1, keepdims=True)
        parts = (
            vcol,
            (icol >> 16).astype(F32),
            ((icol >> 8) & 255).astype(F32),
            (icol & 255).astype(F32),
        )
        for q, part in enumerate(parts):
            cols = jnp.where(lane == 4 * t + q, part, cols)
    top = rows[...].astype(BF16)
    low = cols.astype(BF16)
    for d in range(out.shape[0]):
        out[d, 0:16, :] = top
        out[d, 16:32, :] = low


def square_kernel(hid, val, sq, hv, sem):
    n = sq.shape[0]
    step = hid.shape[0] // n
    copies = []
    for d in range(n):
        where = pl.ds(d * step, step)
        copies.append(pltpu.make_async_copy(hid.at[where, :], hv.at[where, :], sem.at[d]))
    for c in copies:
        c.start()
    ones = (lax.broadcasted_iota(jnp.int32, (8, hid.shape[1]), 0) == 0).astype(BF16)
    srow = lax.broadcasted_iota(jnp.int32, (8, step), 0)
    for d in range(n):
        copies[d].wait()
        h = hv[d * step : (d + 1) * step, :].astype(F32)
        s = h * h
        hi = s.astype(BF16)
        lo = (s - hi.astype(F32)).astype(BF16)
        dims = (((1,), (1,)), ((), ()))
        acc = lax.dot_general(ones, hi, dims, preferred_element_type=F32)
        acc = acc + lax.dot_general(ones, lo, dims, preferred_element_type=F32)
        v = val[:, d * step : (d + 1) * step].astype(F32)
        acc = acc + jnp.where(srow == 1, jnp.sum(v * v, axis=0, keepdims=True), 0.0)
        sq[d] = acc


def inner_kernel(centers, got, hid, val, ids, sq, out, cvec, idb, vb):
    n, _, step = sq.shape
    width = hid.shape[1]
    chunks = width // LANES
    rows_all = hid.shape[0]
    lane = lax.broadcasted_iota(jnp.int32, (K_LOC, LANES), 1)
    cvec[...] = jnp.zeros_like(cvec)
    norms = []
    for t in range(STEPS):
        owner = centers[t] // rows_all
        tile = got[owner].astype(F32)
        for j in range(chunks):
            r = t * chunks + j
            cvec[2 + t : 3 + t, j * LANES : (j + 1) * LANES] = tile[r : r + 1, :]
        low = tile[16:32, :]
        cs = [jnp.sum(jnp.where(lane == 4 * t + q, low, 0.0), axis=1, keepdims=True) for q in range(4)]
        idc = (cs[1] * 65536.0 + cs[2] * 256.0 + cs[3]).astype(jnp.int32)
        idb[t] = jnp.broadcast_to(idc, (K_LOC, LANES))
        vb[t] = jnp.broadcast_to(cs[0], (K_LOC, LANES))
        norms.append(jnp.sum(cs[0] * cs[0], axis=0, keepdims=True))
    cmat = cvec[...]
    crow = lax.broadcasted_iota(jnp.int32, (8, LANES), 0)
    tail = jnp.broadcast_to(jnp.sum(cmat * cmat, axis=1, keepdims=True), (8, LANES))
    for t in range(STEPS):
        tail = jnp.where(crow == 2 + STEPS + t, norms[t], tail)
    cb = cmat.astype(BF16)
    srow = lax.broadcasted_iota(jnp.int32, (8, step), 0)
    for d in range(n):
        part = slice(d * step, (d + 1) * step)
        acc = lax.dot_general(
            cb, hid[part, :], (((1,), (1,)), ((), ())), preferred_element_type=F32
        )
        acc = acc + sq[d]
        ident = ids[:, part]
        vals = val[:, part].astype(F32)
        for t in range(STEPS):
            w = jnp.zeros((K_LOC, step), F32)
            for l in range(K_LOC):
                idl = jnp.broadcast_to(idb[t, l : l + 1, 0:1], (K_LOC, step))
                vl = jnp.broadcast_to(vb[t, l : l + 1, 0:1], (K_LOC, step))
                w = jnp.where(ident == idl, vl, w)
            aa = jnp.sum(w * vals, axis=0, keepdims=True)
            acc = jnp.where(srow == 2 + STEPS + t, aa, acc)
        out[d, :, 0:step] = acc
        out[d, :, step:] = tail


def dist_kernel(parts, mind, sums):
    step = mind.shape[1]
    s = parts[0]
    for d in range(1, parts.shape[0]):
        s = s + parts[d]
    sq = s[0:1, 0:step] * s[1:2, 0:step]
    lane = lax.broadcasted_iota(jnp.int32, (1, LANES), 1)
    row = jnp.zeros((1, LANES), F32)
    low = None
    for t in range(STEPS):
        a, b = 2 + t, 2 + STEPS + t
        norm = s[a : a + 1, step : step + 1] * s[b : b + 1, step : step + 1]
        dist = sq + norm - 2.0 * s[a : a + 1, 0:step] * s[b : b + 1, 0:step]
        dist = jnp.maximum(dist, 0.0)
        low = dist if t == 0 else jnp.minimum(low, dist)
        row = jnp.where(lane == t, jnp.sum(low, axis=1, keepdims=True), row)
    mind[...] = low
    sums[...] = jnp.broadcast_to(row, sums.shape)


def body(hidden_states, factor_values, class_ids, centers):
    rows_all, width = hidden_states.shape
    n_dp, n_mp = lax.axis_size(DP), lax.axis_size(MP)
    n_all = n_dp * n_mp
    rows = rows_all // n_mp
    val = factor_values.T
    ids = class_ids.T
    anyspec = pl.BlockSpec(memory_space=pl.ANY)
    smem = pl.BlockSpec(memory_space=pltpu.SMEM)

    picked = pl.pallas_call(
        pick_kernel,
        out_shape=jax.ShapeDtypeStruct((n_dp, 32, LANES), BF16),
        in_specs=[smem, anyspec, anyspec, anyspec],
        out_specs=vspec(),
        scratch_shapes=[
            VMEM((STEPS, 8, width), BF16),
            VMEM((STEPS, K_LOC, LANES), BF16),
            VMEM((STEPS, K_LOC, LANES), jnp.int32),
            VMEM((16, LANES), F32),
            pltpu.SemaphoreType.DMA((STEPS, 3)),
        ],
        compiler_params=params(4),
    )(centers, hidden_states, val, ids)
    got = lax.all_to_all(picked, DP, 0, 0, tiled=True)

    sq, held = pl.pallas_call(
        square_kernel,
        out_shape=[
            jax.ShapeDtypeStruct((n_mp, 8, rows), F32),
            VMEM((rows_all, width), BF16),
        ],
        in_specs=[anyspec, vspec()],
        out_specs=[vspec(), vspec()],
        scratch_shapes=[pltpu.SemaphoreType.DMA((n_mp,))],
        compiler_params=params(24),
        cost_estimate=pl.CostEstimate(flops=8 * rows_all * width * 4, bytes_accessed=rows_all * width * 2, transcendentals=0),
    )(hidden_states, val)

    parts = pl.pallas_call(
        inner_kernel,
        out_shape=jax.ShapeDtypeStruct((n_mp, 8, rows + LANES), F32),
        in_specs=[smem] + [vspec()] * 5,
        out_specs=vspec(),
        scratch_shapes=[
            VMEM((8, width), F32),
            VMEM((STEPS, K_LOC, LANES), jnp.int32),
            VMEM((STEPS, K_LOC, LANES), F32),
        ],
        compiler_params=params(24),
    )(centers, got, held, val, ids, sq)
    parts = lax.all_to_all(parts, MP, 0, 0, tiled=True)

    mind, sums = pl.pallas_call(
        dist_kernel,
        out_shape=[
            jax.ShapeDtypeStruct((1, rows), F32),
            jax.ShapeDtypeStruct((n_all, LANES), F32),
        ],
        in_specs=[vspec()],
        out_specs=[vspec(), vspec()],
        compiler_params=params(4),
    )(parts)
    sums = lax.all_to_all(sums, DP_MP, 0, 0, tiled=True)
    means = jnp.sum(sums, axis=0)[:STEPS] / (rows_all * n_dp)
    return mind.reshape(rows), means


def solution(mesh):
    finer = Mesh(mesh.devices.reshape(2, 4, 2, 4, 2), DP_MP)
    return jax.shard_map(
        body,
        mesh=finer,
        in_specs=(P(DP, MP), P(DP, MP), P(DP, MP), P()),
        out_specs=(P(DP_MP), P()),
        check_vma=False,
    )
```

time: 138 us -> 58.5 us (0.42)
  blocking collectives: 101 us -> 30.3 us
  other arithmetic: 14.5 us -> 0.67 us
  Pallas kernels: 0 us -> 7.88 us
  between operations: 4.63 us -> 0.7 us
  starting transfers between devices: 3.37 us -> 7.16 us
  matrix products: 3.36 us -> 0 us
  waiting for transfers between devices: 1.83 us -> 0.04 us
  local copies, waits for them, and re-layouts: 9.23 us -> 11 us
    psum x6 -> x0, blocking collectives: 101 us -> none  [the longest x1 68.8 us: body(): table_h, table_v, table_i = lax.psum((table_h, table_v, table_i), DP_MP)]
    all_to_all x0 -> x2, blocking collectives: none -> 30.3 us  [the longest x1 18.2 us: body(): sums = lax.all_to_all(sums, DP_MP, 0, 0, tiled=True)]
    reduce_sum x9 -> x1, other arithmetic: 8.8 us -> 0.15 us  [body(): means = jnp.sum(sums, axis=0)[:STEPS] / (rows_all * n_dp)]
    unnamed x6 -> x20, local copies, waits for them, and re-layouts: 2.94 us -> 11 us
    pallas_call x0 -> x4, Pallas kernels: none -> 7.88 us  [the longest x1 3.79 us: body(): pl.pallas_call(square_kernel, out_shape=[jax.ShapeDtypeStruct((n_mp, 8, r...]
    gather x3 -> x0, local copies, waits for them, and re-layouts: 4.41 us -> none  [the longest x1 3.29 us: body(): pick_h = hidden_states[offsets].astype(jnp.float32) * mine]
    all_to_all x1, starting transfers between devices: 3.37 us -> 7.16 us  [body(): got = lax.all_to_all(picked, DP, 0, 0, tiled=True)]
    dot_general x1 -> x0, matrix products: 3.36 us -> none  [body(): jnp.dot(hidden_states, local_h.T, preferred_element_type=jnp.float32)]
  transfers between devices with their start and end apart: 1 -> 1, of which waited for: 1 -> 0; matrix products, arithmetic and copies ran while one was open for 1% -> 0% of each run, Pallas kernels for 0% -> 7%
where the time goes in v1:
time: 58.5 us; the launch traced here: 57.7 us
  blocking collectives  30.3 us (52%)
  local copies, waits for them, and re-layouts  11 us (19%)
  Pallas kernels  7.88 us (13%)
  starting transfers between devices  7.16 us (12%)
  between operations  0.7 us (1%)
  other arithmetic  0.67 us (1%)
    all_to_all x1, blocking collectives, body(): sums = lax.all_to_all(sums, DP_MP, 0, 0, tiled=True)  18.2 us
    all_to_all x1, blocking collectives, body(): parts = lax.all_to_all(parts, MP, 0, 0, tiled=True)  12.1 us
    unnamed x20, local copies, waits for them, and re-layouts  11 us
    all_to_all x1, starting transfers between devices, body(): got = lax.all_to_all(picked, DP, 0, 0, tiled=True)  7.16 us
    pallas_call x1, Pallas kernels, body(): pl.pallas_call(square_kernel, out_shape=[jax.ShapeDtypeStruct((n_mp, 8, r...  3.79 us
    pallas_call x1, Pallas kernels, body(): pl.pallas_call(inner_kernel, out_shape=jax.ShapeDtypeStruct((n_mp, 8, row...  1.93 us
    pallas_call x1, Pallas kernels, body(): pl.pallas_call(pick_kernel, out_shape=jax.ShapeDtypeStruct((n_dp, 32, LAN...  1.49 us
  transfers between devices with their start and end apart: 1, of which 0 were waited for; matrix products, arithmetic and copies ran while one was open for 0% of the time, Pallas kernels for 7%

profile of v1, /device:TPU:0, one launch (start us, length us, event | category | flops | bytes accessed | tf_op | source)
XLA Modules:
  0.0 57.7 jit_solution(11944905817343131520)
XLA Ops:
  0.6 0.0 copy-start
  0.6 2.2 %copy-done = bf16[4096,512]{1,0:T(8,128)(2,1)S(1)} copy-done((bf16[4096,512]{1,0:T(8,128)(2,1)S(1)}, bf16[4096,512]{1,0:T(8,128)(2,1)}, u32[]{:S(2)}) %copy-start) | copy-done | bytes 4194328
  2.8 0.0 copy-start.4
  2.8 0.9 %copy-done.4 = bf16[4096,16]{0,1:T(8,128)(2,1)S(1)} copy-done((bf16[4096,16]{0,1:T(8,128)(2,1)S(1)}, bf16[4096,16]{0,1:T(8,128)(2,1)}, u32[]{:S(2)}) %copy-start.4) | copy-done | bytes 131096
  3.7 0.9 %copy-done.6 = s32[4096,16]{0,1:T(8,128)S(1)} copy-done((s32[4096,16]{0,1:T(8,128)S(1)}, s32[4096,16]{0,1:T(8,128)}, u32[]{:S(2)}) %copy-start.6) | copy-done | bytes 262168
  4.7 0.7 %copy-done.8 = s32[3]{0:T(128)S(1)} copy-done((s32[3]{0:T(128)S(1)}, s32[3]{0:T(128)}, u32[]{:S(2)}) %copy-start.8) | copy-done | bytes 36
  5.3 1.5 %shard_map.59 = bf16[16,32,128]{2,1,0:T(8,128)(2,1)} custom-call(s32[3]{0:T(128)S(1)} %copy-done.8, bf16[4096,512]{1,0:T(8,128)(2,1)S(1)} %copy-done, bf16[16,4096]{1,0:T(8,128)(2,1)S(1)} %bitcast.6, s32[16,4096]{1,0:T(8,128)S(1)} %bitcast.9), custom_call_target="tpu_custom_call" | custom-call | tf_op jit(solution)/shard_map/pallas_call | solution.py:175
  6.8 7.2 %all-to-all-start = ((bf16[16,32,128]{2,1,0:T(8,128)(2,1)}), bf16[16,32,128]{2,1,0:T(8,128)(2,1)S(1)}, u32[]{:S(2)}, u32[]{:S(2)}) async-start(bf16[16,32,128]{2,1,0:T(8,128)(2,1)} %shard_map.59), calls=%async_computation | async-start | bytes 262144 | tf_op jit(solution)/shard_map/all_to_all | solution.py:189
  14.0 0.0 copy-done.5
  14.0 0.0 copy-start.1
  14.0 2.2 %copy-done.1 = bf16[4096,512]{1,0:T(8,128)(2,1)S(1)} copy-done((bf16[4096,512]{1,0:T(8,128)(2,1)S(1)}, bf16[4096,512]{1,0:T(8,128)(2,1)}, u32[]{:S(2)}) %copy-start.1) | copy-done | bytes 4194328
  16.2 3.8 %shard_map.60 = (f32[8,8,512]{2,1,0:T(8,128)S(1)}, bf16[4096,512]{1,0:T(8,128)(2,1)S(1)}) custom-call(bf16[4096,512]{1,0:T(8,128)(2,1)S(1)} %copy-done.1, bf16[16,4096]{1,0:T(8,128)(2,1)S(1)} %bitcast.7), custom_call_target="tpu_custom_call" | custom-call | flops 67108864 | bytes 4194304 | tf_op jit(solution)/shard_map/pallas_call | solution.py:191
  20.0 0.0 copy-start.2
  20.0 1.9 %copy-done.2 = bf16[4096,512]{1,0:T(8,128)(2,1)} copy-done((bf16[4096,512]{1,0:T(8,128)(2,1)}, bf16[4096,512]{1,0:T(8,128)(2,1)S(1)}, u32[]{:S(2)}) %copy-start.2) | copy-done | bytes 4194328
  22.0 0.0 all-to-all-done.got
  22.0 0.0 copy-done.7
  22.0 0.0 copy-done.9
  22.0 2.2 %copy-done.3 = bf16[4096,512]{1,0:T(8,128)(2,1)S(1)} copy-done((bf16[4096,512]{1,0:T(8,128)(2,1)S(1)}, bf16[4096,512]{1,0:T(8,128)(2,1)}, u32[]{:S(2)}) %copy-start.3) | copy-done | bytes 4194328
  24.2 1.9 %shard_map.61 = f32[8,8,640]{2,1,0:T(8,128)S(1)} custom-call(s32[3]{0:T(128)S(1)} %copy-done.9, bf16[16,32,128]{2,1,0:T(8,128)(2,1)S(1)} %all-to-all-done.got, bf16[4096,512]{1,0:T(8,128)(2,1)S(1)} %copy-done.3, bf16[16,4096]{1,0:T(8,128)(2,1)S(1)} %bitcast.8, s32[16,4096]{1,0:T(8,128)S(1)} %bitcast.10, f32[8,8,512]{2,1,0:T(8,128)S(1)} %get-tuple-element.7.sq), custom_call_target="tpu_custom_call" | custom-call | tf_op jit(solution)/shard_map/pallas_call | solution.py:204
  26.1 12.1 %all_to_all.19.parts = f32[8,8,640]{2,1,0:T(8,128)S(1)} all-to-all(f32[8,8,640]{2,1,0:T(8,128)S(1)} %shard_map.61), channel_id=1, replica_groups=mesh['dp_0'=2,'dp_1'=4,'dp_2'=2,'mp_0'=4,'mp_1'=2] {'mp_0','mp_1'}, dimensions={0} | all-to-all | bytes 327680 | tf_op jit(solution)/shard_map/all_to_all | solution.py:216
  38.2 0.7 %shard_map.62 = (f32[1,512]{1,0:T(1,128)}, f32[128,128]{1,0:T(8,128)S(1)}) custom-call(f32[8,8,640]{2,1,0:T(8,128)S(1)} %all_to_all.19.parts), custom_call_target="tpu_custom_call" | custom-call | tf_op jit(solution)/shard_map/pallas_call | solution.py:218
  38.9 18.2 %all_to_all.20 = f32[128,1,128]{2,1,0:T(1,128)S(1)} all-to-all(f32[128,1,128]{2,1,0:T(1,128)S(1)} %bitcast.11), channel_id=1, replica_groups=mesh['dp_0'=2,'dp_1'=4,'dp_2'=2,'mp_0'=4,'mp_1'=2] {'dp_0','dp_1','dp_2'..., dimensions={0} | all-to-all | bytes 131072 | tf_op jit(solution)/shard_map/all_to_all | solution.py:228
  57.1 0.2 reduce_sum.9
  57.2 0.5 slice_multiply_fusion
  (6 shorter events, 0.0 us)
Async XLA Ops:
  0.6 2.2 %copy-start = (bf16[4096,512]{1,0:T(8,128)(2,1)S(1)}, bf16[4096,512]{1,0:T(8,128)(2,1)}, u32[]{:S(2)}) copy-start(bf16[4096,512]{1,0:T(8,128)(2,1)} %hid.3) | copy-start | bytes 12582916
  2.8 0.9 %copy-start.4 = (bf16[4096,16]{0,1:T(8,128)(2,1)S(1)}, bf16[4096,16]{0,1:T(8,128)(2,1)}, u32[]{:S(2)}) copy-start(bf16[4096,16]{0,1:T(8,128)(2,1)} %param.5) | copy-start | bytes 393220
  3.7 0.9 %copy-start.6 = (s32[4096,16]{0,1:T(8,128)S(1)}, s32[4096,16]{0,1:T(8,128)}, u32[]{:S(2)}) copy-start(s32[4096,16]{0,1:T(8,128)} %param.6) | copy-start | bytes 786436
  4.7 0.7 %copy-start.8 = (s32[3]{0:T(128)S(1)}, s32[3]{0:T(128)}, u32[]{:S(2)}) copy-start(s32[3]{0:T(128)} %centers.3) | copy-start | bytes 40
  5.3 8.7 %copy-start.5 = (bf16[4096,16]{0,1:T(8,128)(2,1)S(1)}, bf16[4096,16]{0,1:T(8,128)(2,1)}, u32[]{:S(2)}) copy-start(bf16[4096,16]{0,1:T(8,128)(2,1)} %param.5) | copy-start | bytes 393220
  5.3 16.7 %copy-start.7 = (s32[4096,16]{0,1:T(8,128)S(1)}, s32[4096,16]{0,1:T(8,128)}, u32[]{:S(2)}) copy-start(s32[4096,16]{0,1:T(8,128)} %param.6) | copy-start | bytes 786436
  5.3 16.7 %copy-start.9 = (s32[3]{0:T(128)S(1)}, s32[3]{0:T(128)}, u32[]{:S(2)}) copy-start(s32[3]{0:T(128)} %centers.3) | copy-start | bytes 40
  6.8 15.2 %all-to-all-start = ((bf16[16,32,128]{2,1,0:T(8,128)(2,1)}), bf16[16,32,128]{2,1,0:T(8,128)(2,1)S(1)}, u32[]{:S(2)}, u32[]{:S(2)}) async-start(bf16[16,32,128]{2,1,0:T(8,128)(2,1)} %shard_map.59), calls=%async_computation | async-start | bytes 262144 | tf_op jit(solution)/shard_map/all_to_all | solution.py:189
  14.0 2.2 %copy-start.1 = (bf16[4096,512]{1,0:T(8,128)(2,1)S(1)}, bf16[4096,512]{1,0:T(8,128)(2,1)}, u32[]{:S(2)}) copy-start(bf16[4096,512]{1,0:T(8,128)(2,1)} %hid.3) | copy-start | bytes 12582916
  20.0 2.0 %copy-start.2 = (bf16[4096,512]{1,0:T(8,128)(2,1)}, bf16[4096,512]{1,0:T(8,128)(2,1)S(1)}, u32[]{:S(2)}) copy-start(bf16[4096,512]{1,0:T(8,128)(2,1)S(1)} %get-tuple-element.6.hid) | copy-start | bytes 12582916
  22.0 2.2 %copy-start.3 = (bf16[4096,512]{1,0:T(8,128)(2,1)S(1)}, bf16[4096,512]{1,0:T(8,128)(2,1)}, u32[]{:S(2)}) copy-start(bf16[4096,512]{1,0:T(8,128)(2,1)} %copy-done.2) | copy-start | bytes 12582916

commit v2 on v1

--- a/solution.py
+++ b/solution.py
@@ -27,11 +27,19 @@
     return pltpu.CompilerParams(vmem_limit_bytes=mib * 1024 * 1024)
 
 
-def pick_kernel(centers, hid, val, ids, out, hbuf, vbuf, ibuf, rows, sem):
+def pick_kernel(centers, hid, val, ids, out, cbuf, hbuf, vbuf, ibuf, rows, csem, sem):
     rows_all = hid.shape[0]
+    first = pltpu.make_async_copy(centers, cbuf, csem)
+    first.start()
+    me = lax.axis_index(DP)
+    chunks = hid.shape[1] // LANES
+    rows[...] = jnp.zeros_like(rows)
+    lane = lax.broadcasted_iota(jnp.int32, (K_LOC, LANES), 1)
+    cols = jnp.zeros((K_LOC, LANES), F32)
+    first.wait()
     copies = []
     for t in range(STEPS):
-        off = lax.rem(centers[t], rows_all)
+        off = lax.rem(cbuf[t], rows_all)
         row8 = pl.multiple_of((off // 8) * 8, 8)
         col = pl.multiple_of((off // LANES) * LANES, LANES)
         copies.append(pltpu.make_async_copy(hid.at[pl.ds(row8, 8), :], hbuf.at[t], sem.at[t, 0]))
@@ -39,20 +47,18 @@
         copies.append(pltpu.make_async_copy(ids.at[:, pl.ds(col, LANES)], ibuf.at[t], sem.at[t, 2]))
     for c in copies:
         c.start()
-    chunks = hid.shape[1] // LANES
-    rows[...] = jnp.zeros_like(rows)
-    lane = lax.broadcasted_iota(jnp.int32, (K_LOC, LANES), 1)
-    cols = jnp.zeros((K_LOC, LANES), F32)
     for c in copies:
         c.wait()
     for t in range(STEPS):
-        off = lax.rem(centers[t], rows_all)
+        mine = cbuf[t] // rows_all == me
+        off = jnp.where(mine, lax.rem(cbuf[t], rows_all), rows_all)
         blk = hbuf[t].astype(F32)
-        here = lax.broadcasted_iota(jnp.int32, blk.shape, 0) == lax.rem(off, 8)
+        srow = lax.broadcasted_iota(jnp.int32, blk.shape, 0)
+        here = srow == jnp.where(mine, lax.rem(off, 8), 8)
         row = jnp.sum(jnp.where(here, blk, 0.0), axis=0, keepdims=True)
         for j in range(chunks):
             rows[t * chunks + j : t * chunks + j + 1, :] = row[:, j * LANES : (j + 1) * LANES]
-        here = lane == lax.rem(off, LANES)
+        here = lane == jnp.where(mine, lax.rem(off, LANES), LANES)
         vcol = jnp.sum(jnp.where(here, vbuf[t].astype(F32), 0.0), axis=1, keepdims=True)
         icol = jnp.sum(jnp.where(here, ibuf[t], 0), axis=1, keepdims=True)
         parts = (
@@ -70,46 +76,21 @@
         out[d, 16:32, :] = low
 
 
-def square_kernel(hid, val, sq, hv, sem):
-    n = sq.shape[0]
+def inner_kernel(got, hid, val, ids, out, cvec, idb, vb):
+    n = out.shape[0]
     step = hid.shape[0] // n
-    copies = []
-    for d in range(n):
-        where = pl.ds(d * step, step)
-        copies.append(pltpu.make_async_copy(hid.at[where, :], hv.at[where, :], sem.at[d]))
-    for c in copies:
-        c.start()
-    ones = (lax.broadcasted_iota(jnp.int32, (8, hid.shape[1]), 0) == 0).astype(BF16)
-    srow = lax.broadcasted_iota(jnp.int32, (8, step), 0)
-    for d in range(n):
-        copies[d].wait()
-        h = hv[d * step : (d + 1) * step, :].astype(F32)
-        s = h * h
-        hi = s.astype(BF16)
-        lo = (s - hi.astype(F32)).astype(BF16)
-        dims = (((1,), (1,)), ((), ()))
-        acc = lax.dot_general(ones, hi, dims, preferred_element_type=F32)
-        acc = acc + lax.dot_general(ones, lo, dims, preferred_element_type=F32)
-        v = val[:, d * step : (d + 1) * step].astype(F32)
-        acc = acc + jnp.where(srow == 1, jnp.sum(v * v, axis=0, keepdims=True), 0.0)
-        sq[d] = acc
-
-
-def inner_kernel(centers, got, hid, val, ids, sq, out, cvec, idb, vb):
-    n, _, step = sq.shape
-    width = hid.shape[1]
-    chunks = width // LANES
-    rows_all = hid.shape[0]
+    chunks = hid.shape[1] // LANES
     lane = lax.broadcasted_iota(jnp.int32, (K_LOC, LANES), 1)
+    tile = got[0].astype(F32)
+    for d in range(1, got.shape[0]):
+        tile = tile + got[d].astype(F32)
+    low = tile[16:32, :]
     cvec[...] = jnp.zeros_like(cvec)
     norms = []
     for t in range(STEPS):
-        owner = centers[t] // rows_all
-        tile = got[owner].astype(F32)
         for j in range(chunks):
             r = t * chunks + j
             cvec[2 + t : 3 + t, j * LANES : (j + 1) * LANES] = tile[r : r + 1, :]
-        low = tile[16:32, :]
         cs = [jnp.sum(jnp.where(lane == 4 * t + q, low, 0.0), axis=1, keepdims=True) for q in range(4)]
         idc = (cs[1] * 65536.0 + cs[2] * 256.0 + cs[3]).astype(jnp.int32)
         idb[t] = jnp.broadcast_to(idc, (K_LOC, LANES))
@@ -121,15 +102,23 @@
     for t in range(STEPS):
         tail = jnp.where(crow == 2 + STEPS + t, norms[t], tail)
     cb = cmat.astype(BF16)
+    ones = (crow == 0).astype(BF16)
     srow = lax.broadcasted_iota(jnp.int32, (8, step), 0)
+    dims = (((1,), (1,)), ((), ()))
     for d in range(n):
         part = slice(d * step, (d + 1) * step)
-        acc = lax.dot_general(
-            cb, hid[part, :], (((1,), (1,)), ((), ())), preferred_element_type=F32
-        )
-        acc = acc + sq[d]
+        acc = lax.dot_general(cb, hid[part, :], dims, preferred_element_type=F32)
+        total = jnp.zeros((step, LANES), F32)
+        for j in range(chunks):
+            h = hid[part, j * LANES : (j + 1) * LANES].astype(F32)
+            total = total + h * h
+        hi = total.astype(BF16)
+        lo = (total - hi.astype(F32)).astype(BF16)
+        acc = acc + lax.dot_general(ones, hi, dims, preferred_element_type=F32)
+        acc = acc + lax.dot_general(ones, lo, dims, preferred_element_type=F32)
         ident = ids[:, part]
         vals = val[:, part].astype(F32)
+        acc = jnp.where(srow == 1, jnp.sum(vals * vals, axis=0, keepdims=True), acc)
         for t in range(STEPS):
             w = jnp.zeros((K_LOC, step), F32)
             for l in range(K_LOC):
@@ -169,42 +158,30 @@
     rows = rows_all // n_mp
     val = factor_values.T
     ids = class_ids.T
-    anyspec = pl.BlockSpec(memory_space=pl.ANY)
-    smem = pl.BlockSpec(memory_space=pltpu.SMEM)
+    hbm = pl.BlockSpec(memory_space=pltpu.HBM)
 
     picked = pl.pallas_call(
         pick_kernel,
         out_shape=jax.ShapeDtypeStruct((n_dp, 32, LANES), BF16),
-        in_specs=[smem, anyspec, anyspec, anyspec],
+        in_specs=[hbm] * 4,
         out_specs=vspec(),
         scratch_shapes=[
+            pltpu.SMEM((STEPS,), jnp.int32),
             VMEM((STEPS, 8, width), BF16),
             VMEM((STEPS, K_LOC, LANES), BF16),
             VMEM((STEPS, K_LOC, LANES), jnp.int32),
             VMEM((16, LANES), F32),
+            pltpu.SemaphoreType.DMA,
             pltpu.SemaphoreType.DMA((STEPS, 3)),
         ],
         compiler_params=params(4),
-    )(centers, hidden_states, val, ids)
+    )(*(pltpu.with_memory_space_constraint(x, pltpu.HBM) for x in (centers, hidden_states, val, ids)))
     got = lax.all_to_all(picked, DP, 0, 0, tiled=True)
-
-    sq, held = pl.pallas_call(
-        square_kernel,
-        out_shape=[
-            jax.ShapeDtypeStruct((n_mp, 8, rows), F32),
-            VMEM((rows_all, width), BF16),
-        ],
-        in_specs=[anyspec, vspec()],
-        out_specs=[vspec(), vspec()],
-        scratch_shapes=[pltpu.SemaphoreType.DMA((n_mp,))],
-        compiler_params=params(24),
-        cost_estimate=pl.CostEstimate(flops=8 * rows_all * width * 4, bytes_accessed=rows_all * width * 2, transcendentals=0),
-    )(hidden_states, val)
 
     parts = pl.pallas_call(
         inner_kernel,
         out_shape=jax.ShapeDtypeStruct((n_mp, 8, rows + LANES), F32),
-        in_specs=[smem] + [vspec()] * 5,
+        in_specs=[vspec()] * 4,
         out_specs=vspec(),
         scratch_shapes=[
             VMEM((8, width), F32),
@@ -212,7 +189,7 @@
             VMEM((STEPS, K_LOC, LANES), F32),
         ],
         compiler_params=params(24),
-    )(centers, got, held, val, ids, sq)
+    )(got, hidden_states, val, ids)
     parts = lax.all_to_all(parts, MP, 0, 0, tiled=True)
 
     mind, sums = pl.pallas_call(

time: 58.5 us -> 47.7 us (0.82)
  local copies, waits for them, and re-layouts: 11 us -> 0.01 us
  blocking collectives: 30.3 us -> 40.6 us
  starting transfers between devices: 7.16 us -> 0 us
  Pallas kernels: 7.88 us -> 5.18 us
    all_to_all x0 -> x1, blocking collectives: none -> 14.9 us  [body(): got = lax.all_to_all(picked, DP, 0, 0, tiled=True)]
    unnamed x20 -> x6, local copies, waits for them, and re-layouts: 11 us -> 0.01 us
    all_to_all x1 -> x0, starting transfers between devices: 7.16 us -> none  [body(): got = lax.all_to_all(picked, DP, 0, 0, tiled=True)]
    all_to_all x1, blocking collectives: 18.2 us -> 13.6 us  [body(): sums = lax.all_to_all(sums, DP_MP, 0, 0, tiled=True)]
    pallas_call x1 -> x0, Pallas kernels: 3.79 us -> none  [body(): pl.pallas_call(square_kernel, out_shape=[jax.ShapeDtypeStruct((n_mp, 8, r...]
    pallas_call x1, Pallas kernels: 1.49 us -> 2.24 us  [body(): pl.pallas_call(pick_kernel, out_shape=jax.ShapeDtypeStruct((n_dp, 32, LAN...]
  transfers between devices with their start and end apart: 1 -> 0, of which waited for: 0 -> 0; matrix products, arithmetic and copies ran while one was open for 0% -> 0% of each run, Pallas kernels for 7% -> 0%
where the time goes in v2:
time: 47.7 us; the launch traced here: 47.2 us
  blocking collectives  40.6 us (85%)
  Pallas kernels  5.18 us (11%)
  between operations  0.68 us (1%)
  other arithmetic  0.67 us (1%)
    all_to_all x1, blocking collectives, body(): got = lax.all_to_all(picked, DP, 0, 0, tiled=True)  14.9 us
    all_to_all x1, blocking collectives, body(): sums = lax.all_to_all(sums, DP_MP, 0, 0, tiled=True)  13.6 us
    all_to_all x1, blocking collectives, body(): parts = lax.all_to_all(parts, MP, 0, 0, tiled=True)  12.1 us
    pallas_call x1, Pallas kernels, body(): pl.pallas_call(inner_kernel, out_shape=jax.ShapeDtypeStruct((n_mp, 8, row...  2.28 us
    pallas_call x1, Pallas kernels, body(): pl.pallas_call(pick_kernel, out_shape=jax.ShapeDtypeStruct((n_dp, 32, LAN...  2.24 us

profile of v2, /device:TPU:0, one launch (start us, length us, event | category | flops | bytes accessed | tf_op | source)
XLA Modules:
  0.0 47.2 jit_solution(11206599584606049282)
XLA Ops:
  0.6 0.0 copy-start
  0.6 0.0 copy-start.1
  0.7 0.0 copy-start.2
  0.7 2.2 %shard_map.59 = bf16[16,32,128]{2,1,0:T(8,128)(2,1)S(1)} custom-call(s32[3]{0:T(128)} %centers.1, bf16[4096,512]{1,0:T(8,128)(2,1)} %hid.3, bf16[16,4096]{1,0:T(8,128)(2,1)} %bitcast.8, s32[16,4096]{1,0:T(8,128)} %bitcast.6), custom_call_target="tpu_custom_call" | custom-call | tf_op jit(solution)/shard_map/pallas_call | solution.py:163
  2.9 14.9 %all_to_all.19.got = bf16[16,32,128]{2,1,0:T(8,128)(2,1)S(1)} all-to-all(bf16[16,32,128]{2,1,0:T(8,128)(2,1)S(1)} %shard_map.59), channel_id=1, replica_groups=mesh['dp_0'=2,'dp_1'=4,'dp_2'=2,'mp_0'=4,'mp_1'=2] {'dp_0','dp_1','dp_2'}, dimensions={0} | all-to-all | bytes 262144 | tf_op jit(solution)/shard_map/all_to_all | solution.py:179
  17.8 0.0 copy-done
  17.8 0.0 copy-done.1
  17.8 0.0 copy-done.2
  17.9 2.3 %shard_map.60 = f32[8,8,640]{2,1,0:T(8,128)S(1)} custom-call(bf16[16,32,128]{2,1,0:T(8,128)(2,1)S(1)} %all_to_all.19.got, bf16[4096,512]{1,0:T(8,128)(2,1)S(1)} %copy-done, bf16[16,4096]{1,0:T(8,128)(2,1)S(1)} %bitcast.9, s32[16,4096]{1,0:T(8,128)S(1)} %bitcast.7), custom_call_target="tpu_custom_call" | custom-call | tf_op jit(solution)/shard_map/pallas_call | solution.py:181
  20.1 12.1 %all_to_all.20.parts = f32[8,8,640]{2,1,0:T(8,128)S(1)} all-to-all(f32[8,8,640]{2,1,0:T(8,128)S(1)} %shard_map.60), channel_id=1, replica_groups=mesh['dp_0'=2,'dp_1'=4,'dp_2'=2,'mp_0'=4,'mp_1'=2] {'mp_0','mp_1'}, dimensions={0} | all-to-all | bytes 327680 | tf_op jit(solution)/shard_map/all_to_all | solution.py:193
  32.2 0.7 %shard_map.61 = (f32[1,512]{1,0:T(1,128)}, f32[128,128]{1,0:T(8,128)S(1)}) custom-call(f32[8,8,640]{2,1,0:T(8,128)S(1)} %all_to_all.20.parts), custom_call_target="tpu_custom_call" | custom-call | tf_op jit(solution)/shard_map/pallas_call | solution.py:195
  32.9 13.6 %all_to_all.21 = f32[128,1,128]{2,1,0:T(1,128)S(1)} all-to-all(f32[128,1,128]{2,1,0:T(1,128)S(1)} %bitcast.10), channel_id=1, replica_groups=mesh['dp_0'=2,'dp_1'=4,'dp_2'=2,'mp_0'=4,'mp_1'=2] {'dp_0','dp_1','dp_2'..., dimensions={0} | all-to-all | bytes 131072 | tf_op jit(solution)/shard_map/all_to_all | solution.py:205
  46.5 0.2 reduce_sum.9
  46.7 0.5 %slice_multiply_fusion = f32[3]{0:T(128)} fusion(f32[128]{0:T(128)S(1)} %reduce_sum.9), kind=kLoop, calls=%fused_computation | loop fusion | flops 3 | bytes 24 | tf_op jit(solution)/shard_map/div | solution.py:206
Async XLA Ops:
  0.6 17.2 %copy-start = (bf16[4096,512]{1,0:T(8,128)(2,1)S(1)}, bf16[4096,512]{1,0:T(8,128)(2,1)}, u32[]{:S(2)}) copy-start(bf16[4096,512]{1,0:T(8,128)(2,1)} %hid.3) | copy-start | bytes 12582916
  0.6 17.2 %copy-start.1 = (s32[4096,16]{0,1:T(8,128)S(1)}, s32[4096,16]{0,1:T(8,128)}, u32[]{:S(2)}) copy-start(s32[4096,16]{0,1:T(8,128)} %param.6) | copy-start | bytes 786436
  0.7 17.2 %copy-start.2 = (bf16[4096,16]{0,1:T(8,128)(2,1)S(1)}, bf16[4096,16]{0,1:T(8,128)(2,1)}, u32[]{:S(2)}) copy-start(bf16[4096,16]{0,1:T(8,128)(2,1)} %param.5) | copy-start | bytes 393220

commit v3 on v2

--- a/solution.py
+++ b/solution.py
@@ -17,6 +17,10 @@
 VMEM = pltpu.VMEM
 F32 = jnp.float32
 BF16 = jnp.bfloat16
+
+
+def led_by(size, first):
+    return [(first + i) % size for i in range(size)]
 
 
 def vspec():
@@ -76,7 +80,7 @@
         out[d, 16:32, :] = low
 
 
-def inner_kernel(got, hid, val, ids, out, cvec, idb, vb):
+def inner_kernel(first, got, hid, val, ids, out, cvec, idb, vb):
     n = out.shape[0]
     step = hid.shape[0] // n
     chunks = hid.shape[1] // LANES
@@ -127,8 +131,9 @@
                 w = jnp.where(ident == idl, vl, w)
             aa = jnp.sum(w * vals, axis=0, keepdims=True)
             acc = jnp.where(srow == 2 + STEPS + t, aa, acc)
-        out[d, :, 0:step] = acc
-        out[d, :, step:] = tail
+        slot = (d - first) % n
+        out[slot, :, 0:step] = acc
+        out[slot, :, step:] = tail
 
 
 def dist_kernel(parts, mind, sums):
@@ -158,6 +163,7 @@
     rows = rows_all // n_mp
     val = factor_values.T
     ids = class_ids.T
+    first = 3 * n_mp // 4
     hbm = pl.BlockSpec(memory_space=pltpu.HBM)
 
     picked = pl.pallas_call(
@@ -176,10 +182,10 @@
         ],
         compiler_params=params(4),
     )(*(pltpu.with_memory_space_constraint(x, pltpu.HBM) for x in (centers, hidden_states, val, ids)))
-    got = lax.all_to_all(picked, DP, 0, 0, tiled=True)
+    got = lax.all_to_all(picked, DP, 0, 0, tiled=True, axis_index_groups=[led_by(n_dp, 3 * n_dp // 4)])
 
     parts = pl.pallas_call(
-        inner_kernel,
+        functools.partial(inner_kernel, first),
         out_shape=jax.ShapeDtypeStruct((n_mp, 8, rows + LANES), F32),
         in_specs=[vspec()] * 4,
         out_specs=vspec(),
@@ -190,7 +196,7 @@
         ],
         compiler_params=params(24),
     )(got, hidden_states, val, ids)
-    parts = lax.all_to_all(parts, MP, 0, 0, tiled=True)
+    parts = lax.all_to_all(parts, MP, 0, 0, tiled=True, axis_index_groups=[led_by(n_mp, first)])
 
     mind, sums = pl.pallas_call(
         dist_kernel,

time: 47.7 us -> 47.6 us (level)
    all_to_all x2, blocking collectives: 27 us -> 22.2 us  [the longest x1 11.2 us: body(): lax.all_to_all(picked, DP, 0, 0, tiled=True, axis_index_groups=[led_by(n_...]
    all_to_all x1, blocking collectives: 13.6 us -> 18.3 us  [body(): sums = lax.all_to_all(sums, DP_MP, 0, 0, tiled=True)]
where the time goes in v3:
time: 47.6 us; the launch traced here: 47.1 us
  blocking collectives  40.6 us (85%)
  Pallas kernels  5.18 us (11%)
  between operations  0.68 us (1%)
  other arithmetic  0.67 us (1%)
    all_to_all x1, blocking collectives, body(): sums = lax.all_to_all(sums, DP_MP, 0, 0, tiled=True)  18.3 us
    all_to_all x1, blocking collectives, body(): lax.all_to_all(picked, DP, 0, 0, tiled=True, axis_index_groups=[led_by(n_...  11.2 us
    all_to_all x1, blocking collectives, body(): lax.all_to_all(parts, MP, 0, 0, tiled=True, axis_index_groups=[led_by(n_m...  11 us
    pallas_call x1, Pallas kernels, body(): pl.pallas_call(functools.partial(inner_kernel, first), out_shape=jax.Shap...  2.28 us
    pallas_call x1, Pallas kernels, body(): pl.pallas_call(pick_kernel, out_shape=jax.ShapeDtypeStruct((n_dp, 32, LAN...  2.24 us

profile of v3, /device:TPU:0, one launch (start us, length us, event | category | flops | bytes accessed | tf_op | source)
XLA Modules:
  0.0 47.1 jit_solution(5025877156183797199)
XLA Ops:
  0.6 0.0 copy-start
  0.6 0.0 copy-start.1
  0.7 0.0 copy-start.2
  0.7 2.2 %shard_map.59 = bf16[16,32,128]{2,1,0:T(8,128)(2,1)S(1)} custom-call(s32[3]{0:T(128)} %centers.1, bf16[4096,512]{1,0:T(8,128)(2,1)} %hid.3, bf16[16,4096]{1,0:T(8,128)(2,1)} %bitcast.8, s32[16,4096]{1,0:T(8,128)} %bitcast.6), custom_call_target="tpu_custom_call" | custom-call | tf_op jit(solution)/shard_map/pallas_call | solution.py:169
  2.9 11.2 %all_to_all.19.got = bf16[16,32,128]{2,1,0:T(8,128)(2,1)S(1)} all-to-all(bf16[16,32,128]{2,1,0:T(8,128)(2,1)S(1)} %shard_map.59), channel_id=1, replica_groups={{96,104,112,120,0,8,16,24,32,40,48,56,64,72,80,88},{97,105,113,121,1,9,..., dimensions={0} | all-to-all | bytes 262144 | tf_op jit(solution)/shard_map/all_to_all | solution.py:185
  14.1 0.0 copy-done
  14.1 0.0 copy-done.1
  14.1 0.0 copy-done.2
  14.1 2.3 %shard_map.60 = f32[8,8,640]{2,1,0:T(8,128)S(1)} custom-call(bf16[16,32,128]{2,1,0:T(8,128)(2,1)S(1)} %all_to_all.19.got, bf16[4096,512]{1,0:T(8,128)(2,1)S(1)} %copy-done, bf16[16,4096]{1,0:T(8,128)(2,1)S(1)} %bitcast.9, s32[16,4096]{1,0:T(8,128)S(1)} %bitcast.7), custom_call_target="tpu_custom_call" | custom-call | tf_op jit(solution)/shard_map/pallas_call | solution.py:187
  16.4 11.0 %all_to_all.20.parts = f32[8,8,640]{2,1,0:T(8,128)S(1)} all-to-all(f32[8,8,640]{2,1,0:T(8,128)S(1)} %shard_map.60), channel_id=1, replica_groups={{6,7,0,1,2,3,4,5},{14,15,8,9,10,11,12,13},{22,23,16,17,18,19,20,21},{30..., dimensions={0} | all-to-all | bytes 327680 | tf_op jit(solution)/shard_map/all_to_all | solution.py:199
  27.4 0.7 %shard_map.61 = (f32[1,512]{1,0:T(1,128)}, f32[128,128]{1,0:T(8,128)S(1)}) custom-call(f32[8,8,640]{2,1,0:T(8,128)S(1)} %all_to_all.20.parts), custom_call_target="tpu_custom_call" | custom-call | tf_op jit(solution)/shard_map/pallas_call | solution.py:201
  28.1 18.3 %all_to_all.21 = f32[128,1,128]{2,1,0:T(1,128)S(1)} all-to-all(f32[128,1,128]{2,1,0:T(1,128)S(1)} %bitcast.10), channel_id=1, replica_groups=mesh['dp_0'=2,'dp_1'=4,'dp_2'=2,'mp_0'=4,'mp_1'=2] {'dp_0','dp_1','dp_2'..., dimensions={0} | all-to-all | bytes 131072 | tf_op jit(solution)/shard_map/all_to_all | solution.py:211
  46.4 0.2 reduce_sum.9
  46.6 0.5 %slice_multiply_fusion = f32[3]{0:T(128)} fusion(f32[128]{0:T(128)S(1)} %reduce_sum.9), kind=kLoop, calls=%fused_computation | loop fusion | flops 3 | bytes 24 | tf_op jit(solution)/shard_map/div | solution.py:212
Async XLA Ops:
  0.6 13.5 %copy-start = (bf16[4096,512]{1,0:T(8,128)(2,1)S(1)}, bf16[4096,512]{1,0:T(8,128)(2,1)}, u32[]{:S(2)}) copy-start(bf16[4096,512]{1,0:T(8,128)(2,1)} %hid.3) | copy-start | bytes 12582916
  0.6 13.5 %copy-start.1 = (s32[4096,16]{0,1:T(8,128)S(1)}, s32[4096,16]{0,1:T(8,128)}, u32[]{:S(2)}) copy-start(s32[4096,16]{0,1:T(8,128)} %param.6) | copy-start | bytes 786436
  0.7 13.5 %copy-start.2 = (bf16[4096,16]{0,1:T(8,128)(2,1)S(1)}, bf16[4096,16]{0,1:T(8,128)(2,1)}, u32[]{:S(2)}) copy-start(bf16[4096,16]{0,1:T(8,128)(2,1)} %param.5) | copy-start | bytes 393220

commit v4 on v3

--- a/solution.py
+++ b/solution.py
@@ -37,47 +37,51 @@
     first.start()
     me = lax.axis_index(DP)
     chunks = hid.shape[1] // LANES
+    out[...] = jnp.zeros_like(out)
     rows[...] = jnp.zeros_like(rows)
     lane = lax.broadcasted_iota(jnp.int32, (K_LOC, LANES), 1)
-    cols = jnp.zeros((K_LOC, LANES), F32)
     first.wait()
-    copies = []
-    for t in range(STEPS):
-        off = lax.rem(cbuf[t], rows_all)
-        row8 = pl.multiple_of((off // 8) * 8, 8)
-        col = pl.multiple_of((off // LANES) * LANES, LANES)
-        copies.append(pltpu.make_async_copy(hid.at[pl.ds(row8, 8), :], hbuf.at[t], sem.at[t, 0]))
-        copies.append(pltpu.make_async_copy(val.at[:, pl.ds(col, LANES)], vbuf.at[t], sem.at[t, 1]))
-        copies.append(pltpu.make_async_copy(ids.at[:, pl.ds(col, LANES)], ibuf.at[t], sem.at[t, 2]))
-    for c in copies:
-        c.start()
-    for c in copies:
-        c.wait()
-    for t in range(STEPS):
-        mine = cbuf[t] // rows_all == me
-        off = jnp.where(mine, lax.rem(cbuf[t], rows_all), rows_all)
-        blk = hbuf[t].astype(F32)
-        srow = lax.broadcasted_iota(jnp.int32, blk.shape, 0)
-        here = srow == jnp.where(mine, lax.rem(off, 8), 8)
-        row = jnp.sum(jnp.where(here, blk, 0.0), axis=0, keepdims=True)
-        for j in range(chunks):
-            rows[t * chunks + j : t * chunks + j + 1, :] = row[:, j * LANES : (j + 1) * LANES]
-        here = lane == jnp.where(mine, lax.rem(off, LANES), LANES)
-        vcol = jnp.sum(jnp.where(here, vbuf[t].astype(F32), 0.0), axis=1, keepdims=True)
-        icol = jnp.sum(jnp.where(here, ibuf[t], 0), axis=1, keepdims=True)
-        parts = (
-            vcol,
-            (icol >> 16).astype(F32),
-            ((icol >> 8) & 255).astype(F32),
-            (icol & 255).astype(F32),
-        )
-        for q, part in enumerate(parts):
-            cols = jnp.where(lane == 4 * t + q, part, cols)
-    top = rows[...].astype(BF16)
-    low = cols.astype(BF16)
-    for d in range(out.shape[0]):
-        out[d, 0:16, :] = top
-        out[d, 16:32, :] = low
+    mine = [cbuf[t] // rows_all == me for t in range(STEPS)]
+
+    @pl.when(functools.reduce(jnp.logical_or, mine))
+    def _():
+        copies = []
+        for t in range(STEPS):
+            off = lax.rem(cbuf[t], rows_all)
+            row8 = pl.multiple_of((off // 8) * 8, 8)
+            col = pl.multiple_of((off // LANES) * LANES, LANES)
+            copies.append(pltpu.make_async_copy(hid.at[pl.ds(row8, 8), :], hbuf.at[t], sem.at[t, 0]))
+            copies.append(pltpu.make_async_copy(val.at[:, pl.ds(col, LANES)], vbuf.at[t], sem.at[t, 1]))
+            copies.append(pltpu.make_async_copy(ids.at[:, pl.ds(col, LANES)], ibuf.at[t], sem.at[t, 2]))
+        for c in copies:
+            c.start()
+        for c in copies:
+            c.wait()
+        cols = jnp.zeros((K_LOC, LANES), F32)
+        for t in range(STEPS):
+            off = lax.rem(cbuf[t], rows_all)
+            blk = hbuf[t].astype(F32)
+            srow = lax.broadcasted_iota(jnp.int32, blk.shape, 0)
+            here = srow == jnp.where(mine[t], lax.rem(off, 8), 8)
+            row = jnp.sum(jnp.where(here, blk, 0.0), axis=0, keepdims=True)
+            for j in range(chunks):
+                rows[t * chunks + j : t * chunks + j + 1, :] = row[:, j * LANES : (j + 1) * LANES]
+            here = lane == jnp.where(mine[t], lax.rem(off, LANES), LANES)
+            vcol = jnp.sum(jnp.where(here, vbuf[t].astype(F32), 0.0), axis=1, keepdims=True)
+            icol = jnp.sum(jnp.where(here, ibuf[t], 0), axis=1, keepdims=True)
+            parts = (
+                vcol,
+                (icol >> 16).astype(F32),
+                ((icol >> 8) & 255).astype(F32),
+                (icol & 255).astype(F32),
+            )
+            for q, part in enumerate(parts):
+                cols = jnp.where(lane == 4 * t + q, part, cols)
+        top = rows[...].astype(BF16)
+        low = cols.astype(BF16)
+        for d in range(out.shape[0]):
+            out[d, 0:16, :] = top
+            out[d, 16:32, :] = low
 
 
 def inner_kernel(first, got, hid, val, ids, out, cvec, idb, vb):
@@ -97,8 +101,9 @@
             cvec[2 + t : 3 + t, j * LANES : (j + 1) * LANES] = tile[r : r + 1, :]
         cs = [jnp.sum(jnp.where(lane == 4 * t + q, low, 0.0), axis=1, keepdims=True) for q in range(4)]
         idc = (cs[1] * 65536.0 + cs[2] * 256.0 + cs[3]).astype(jnp.int32)
-        idb[t] = jnp.broadcast_to(idc, (K_LOC, LANES))
-        vb[t] = jnp.broadcast_to(cs[0], (K_LOC, LANES))
+        for l in range(K_LOC):
+            idb[t * K_LOC + l] = jnp.broadcast_to(idc[l : l + 1, :], (K_LOC, LANES)).astype(jnp.int16)
+            vb[t * K_LOC + l] = jnp.broadcast_to(cs[0][l : l + 1, :], (K_LOC, LANES)).astype(BF16)
         norms.append(jnp.sum(cs[0] * cs[0], axis=0, keepdims=True))
     cmat = cvec[...]
     crow = lax.broadcasted_iota(jnp.int32, (8, LANES), 0)
@@ -109,27 +114,29 @@
     ones = (crow == 0).astype(BF16)
     srow = lax.broadcasted_iota(jnp.int32, (8, step), 0)
     dims = (((1,), (1,)), ((), ()))
+    tiles = step // LANES
     for d in range(n):
         part = slice(d * step, (d + 1) * step)
         acc = lax.dot_general(cb, hid[part, :], dims, preferred_element_type=F32)
-        total = jnp.zeros((step, LANES), F32)
+        total = None
         for j in range(chunks):
             h = hid[part, j * LANES : (j + 1) * LANES].astype(F32)
-            total = total + h * h
+            total = h * h if total is None else total + h * h
         hi = total.astype(BF16)
         lo = (total - hi.astype(F32)).astype(BF16)
         acc = acc + lax.dot_general(ones, hi, dims, preferred_element_type=F32)
         acc = acc + lax.dot_general(ones, lo, dims, preferred_element_type=F32)
-        ident = ids[:, part]
+        ident = ids[:, part].astype(jnp.int16)
         vals = val[:, part].astype(F32)
         acc = jnp.where(srow == 1, jnp.sum(vals * vals, axis=0, keepdims=True), acc)
         for t in range(STEPS):
-            w = jnp.zeros((K_LOC, step), F32)
+            w = [jnp.zeros((K_LOC, LANES), BF16)] * tiles
             for l in range(K_LOC):
-                idl = jnp.broadcast_to(idb[t, l : l + 1, 0:1], (K_LOC, step))
-                vl = jnp.broadcast_to(vb[t, l : l + 1, 0:1], (K_LOC, step))
-                w = jnp.where(ident == idl, vl, w)
-            aa = jnp.sum(w * vals, axis=0, keepdims=True)
+                idl = idb[t * K_LOC + l]
+                vl = vb[t * K_LOC + l]
+                w = [jnp.where(ident[:, k * LANES : (k + 1) * LANES] == idl, vl, w[k]) for k in range(tiles)]
+            w = jnp.concatenate(w, axis=1)
+            aa = jnp.sum(w.astype(F32) * vals, axis=0, keepdims=True)
             acc = jnp.where(srow == 2 + STEPS + t, aa, acc)
         slot = (d - first) % n
         out[slot, :, 0:step] = acc
@@ -156,6 +163,12 @@
     sums[...] = jnp.broadcast_to(row, sums.shape)
 
 
+def mean_kernel(pool, sums, mind, out, low):
+    low[...] = mind[...]
+    total = jnp.sum(sums[...], axis=0) / pool
+    out[...] = total[0 : out.shape[0]]
+
+
 def body(hidden_states, factor_values, class_ids, centers):
     rows_all, width = hidden_states.shape
     n_dp, n_mp = lax.axis_size(DP), lax.axis_size(MP)
@@ -191,8 +204,8 @@
         out_specs=vspec(),
         scratch_shapes=[
             VMEM((8, width), F32),
-            VMEM((STEPS, K_LOC, LANES), jnp.int32),
-            VMEM((STEPS, K_LOC, LANES), F32),
+            VMEM((STEPS * K_LOC, K_LOC, LANES), jnp.int16),
+            VMEM((STEPS * K_LOC, K_LOC, LANES), BF16),
         ],
         compiler_params=params(24),
     )(got, hidden_states, val, ids)
@@ -201,7 +214,7 @@
     mind, sums = pl.pallas_call(
         dist_kernel,
         out_shape=[
-            jax.ShapeDtypeStruct((1, rows), F32),
+            VMEM((1, rows), F32),
             jax.ShapeDtypeStruct((n_all, LANES), F32),
         ],
         in_specs=[vspec()],
@@ -209,7 +222,13 @@
         compiler_params=params(4),
     )(parts)
     sums = lax.all_to_all(sums, DP_MP, 0, 0, tiled=True)
-    means = jnp.sum(sums, axis=0)[:STEPS] / (rows_all * n_dp)
+    means, mind = pl.pallas_call(
+        functools.partial(mean_kernel, rows_all * n_dp),
+        out_shape=[jax.ShapeDtypeStruct((STEPS,), F32), jax.ShapeDtypeStruct((1, rows), F32)],
+        in_specs=[vspec(), vspec()],
+        out_specs=[vspec(), vspec()],
+        compiler_params=params(4),
+    )(sums, mind)
     return mind.reshape(rows), means
 
 

time: 47.6 us -> 45.9 us (0.964)
  the two profiles are of different devices: /device:TPU:0 before, /device:TPU:1 now
where the time goes in v4:
time: 45.9 us; the launch traced here: 45.3 us
  blocking collectives  41 us (89%)
  Pallas kernels  3.58 us (8%)
  between operations  0.67 us (1%)
    all_to_all x1, blocking collectives, body(): sums = lax.all_to_all(sums, DP_MP, 0, 0, tiled=True)  18.8 us
    all_to_all x1, blocking collectives, body(): lax.all_to_all(picked, DP, 0, 0, tiled=True, axis_index_groups=[led_by(n_...  12.3 us
    all_to_all x1, blocking collectives, body(): lax.all_to_all(parts, MP, 0, 0, tiled=True, axis_index_groups=[led_by(n_m...  9.92 us
    pallas_call x1, Pallas kernels, body(): pl.pallas_call(functools.partial(inner_kernel, first), out_shape=jax.Shap...  1.92 us

profile of v4, /device:TPU:1, one launch (start us, length us, event | category | flops | bytes accessed | tf_op | source)
XLA Modules:
  0.0 45.3 jit_solution(6900125838520939182)
XLA Ops:
  0.6 0.0 copy-start
  0.6 0.0 copy-start.1
  0.7 0.0 copy-start.2
  0.7 0.9 %shard_map.59 = bf16[16,32,128]{2,1,0:T(8,128)(2,1)S(1)} custom-call(s32[3]{0:T(128)} %centers.1, bf16[4096,512]{1,0:T(8,128)(2,1)} %hid.3, bf16[16,4096]{1,0:T(8,128)(2,1)} %bitcast.9, s32[16,4096]{1,0:T(8,128)} %bitcast.7), custom_call_target="tpu_custom_call" | custom-call | tf_op jit(solution)/shard_map/pallas_call | solution.py:182
  1.6 12.3 %all_to_all.21.got = bf16[16,32,128]{2,1,0:T(8,128)(2,1)S(1)} all-to-all(bf16[16,32,128]{2,1,0:T(8,128)(2,1)S(1)} %shard_map.59), channel_id=1, replica_groups={{96,104,112,120,0,8,16,24,32,40,48,56,64,72,80,88},{97,105,113,121,1,9,..., dimensions={0} | all-to-all | bytes 262144 | tf_op jit(solution)/shard_map/all_to_all | solution.py:198
  13.9 0.0 copy-done
  13.9 0.0 copy-done.1
  13.9 0.0 copy-done.2
  13.9 1.9 %shard_map.60 = f32[8,8,640]{2,1,0:T(8,128)S(1)} custom-call(bf16[16,32,128]{2,1,0:T(8,128)(2,1)S(1)} %all_to_all.21.got, bf16[4096,512]{1,0:T(8,128)(2,1)S(1)} %copy-done, bf16[16,4096]{1,0:T(8,128)(2,1)S(1)} %bitcast.10, s32[16,4096]{1,0:T(8,128)S(1)} %bitcast.8), custom_call_target="tpu_custom_call" | custom-call | tf_op jit(solution)/shard_map/pallas_call | solution.py:200
  15.8 9.9 %all_to_all.22.parts = f32[8,8,640]{2,1,0:T(8,128)S(1)} all-to-all(f32[8,8,640]{2,1,0:T(8,128)S(1)} %shard_map.60), channel_id=1, replica_groups={{6,7,0,1,2,3,4,5},{14,15,8,9,10,11,12,13},{22,23,16,17,18,19,20,21},{30..., dimensions={0} | all-to-all | bytes 327680 | tf_op jit(solution)/shard_map/all_to_all | solution.py:212
  25.8 0.2 shard_map.61
  25.9 18.8 %all_to_all.23 = f32[128,1,128]{2,1,0:T(1,128)S(1)} all-to-all(f32[128,1,128]{2,1,0:T(1,128)S(1)} %bitcast.12), channel_id=1, replica_groups=mesh['dp_0'=2,'dp_1'=4,'dp_2'=2,'mp_0'=4,'mp_1'=2] {'dp_0','dp_1','dp_2'..., dimensions={0} | all-to-all | bytes 131072 | tf_op jit(solution)/shard_map/all_to_all | solution.py:224
  44.7 0.6 %shard_map.62 = (f32[3]{0:T(128)}, f32[1,512]{1,0:T(1,128)}) custom-call(f32[128,128]{1,0:T(8,128)S(1)} %bitcast.11, f32[1,512]{1,0:T(1,128)S(1)} %get-tuple-element.7.mind), custom_call_target="tpu_custom_call" | custom-call | tf_op jit(solution)/shard_map/pallas_call | solution.py:225
Async XLA Ops:
  0.6 13.3 %copy-start = (bf16[4096,512]{1,0:T(8,128)(2,1)S(1)}, bf16[4096,512]{1,0:T(8,128)(2,1)}, u32[]{:S(2)}) copy-start(bf16[4096,512]{1,0:T(8,128)(2,1)} %hid.3) | copy-start | bytes 12582916
  0.6 13.3 %copy-start.1 = (s32[4096,16]{0,1:T(8,128)S(1)}, s32[4096,16]{0,1:T(8,128)}, u32[]{:S(2)}) copy-start(s32[4096,16]{0,1:T(8,128)} %param.6) | copy-start | bytes 786436
  0.7 13.3 %copy-start.2 = (bf16[4096,16]{0,1:T(8,128)(2,1)S(1)}, bf16[4096,16]{0,1:T(8,128)(2,1)}, u32[]{:S(2)}) copy-start(bf16[4096,16]{0,1:T(8,128)(2,1)} %param.5) | copy-start | bytes 393220

commit v5 on v4

--- a/solution.py
+++ b/solution.py
@@ -163,6 +163,10 @@
     sums[...] = jnp.broadcast_to(row, sums.shape)
 
 
+def pair_kernel(own, other, sums):
+    sums[...] = jnp.broadcast_to(own[0:1, :] + other[0:1, :], sums.shape)
+
+
 def mean_kernel(pool, sums, mind, out, low):
     low[...] = mind[...]
     total = jnp.sum(sums[...], axis=0) / pool
@@ -176,7 +180,7 @@
     rows = rows_all // n_mp
     val = factor_values.T
     ids = class_ids.T
-    first = 3 * n_mp // 4
+    first = 6
     hbm = pl.BlockSpec(memory_space=pltpu.HBM)
 
     picked = pl.pallas_call(
@@ -195,7 +199,7 @@
         ],
         compiler_params=params(4),
     )(*(pltpu.with_memory_space_constraint(x, pltpu.HBM) for x in (centers, hidden_states, val, ids)))
-    got = lax.all_to_all(picked, DP, 0, 0, tiled=True, axis_index_groups=[led_by(n_dp, 3 * n_dp // 4)])
+    got = lax.all_to_all(picked, DP, 0, 0, tiled=True, axis_index_groups=[led_by(n_dp, 13)])
 
     parts = pl.pallas_call(
         functools.partial(inner_kernel, first),
@@ -215,13 +219,21 @@
         dist_kernel,
         out_shape=[
             VMEM((1, rows), F32),
-            jax.ShapeDtypeStruct((n_all, LANES), F32),
+            jax.ShapeDtypeStruct((8, LANES), F32),
         ],
         in_specs=[vspec()],
         out_specs=[vspec(), vspec()],
         compiler_params=params(4),
     )(parts)
-    sums = lax.all_to_all(sums, DP_MP, 0, 0, tiled=True)
+    other = lax.ppermute(sums, "dp_2", [(0, 1), (1, 0)])
+    sums = pl.pallas_call(
+        pair_kernel,
+        out_shape=jax.ShapeDtypeStruct((n_all // 2, LANES), F32),
+        in_specs=[vspec(), vspec()],
+        out_specs=vspec(),
+        compiler_params=params(4),
+    )(sums, other)
+    sums = lax.all_to_all(sums, ("dp_0", "dp_1", "mp_0", "mp_1"), 0, 0, tiled=True, axis_index_groups=[led_by(n_all // 2, 54)])
     means, mind = pl.pallas_call(
         functools.partial(mean_kernel, rows_all * n_dp),
         out_shape=[jax.ShapeDtypeStruct((STEPS,), F32), jax.ShapeDtypeStruct((1, rows), F32)],

time: 45.9 us -> 42.4 us (0.924)
  the two profiles are of different devices: /device:TPU:1 before, /device:TPU:0 now
where the time goes in v5:
time: 42.4 us; the launch traced here: 42.2 us
  blocking collectives  36.7 us (87%)
  Pallas kernels  3.58 us (8%)
  waiting for transfers between devices  1.15 us (3%)
  between operations  0.68 us (2%)
    all_to_all x1, blocking collectives, body(): lax.all_to_all(sums, ('dp_0', 'dp_1', 'mp_0', 'mp_1'), 0, 0, tiled=True,...  13.6 us
    all_to_all x1, blocking collectives, body(): lax.all_to_all(picked, DP, 0, 0, tiled=True, axis_index_groups=[led_by(n_...  12.1 us
    all_to_all x1, blocking collectives, body(): lax.all_to_all(parts, MP, 0, 0, tiled=True, axis_index_groups=[led_by(n_m...  11 us
    pallas_call x1, Pallas kernels, body(): pl.pallas_call(functools.partial(inner_kernel, first), out_shape=jax.Shap...  1.92 us
    ppermute x1, waiting for transfers between devices, body(): other = lax.ppermute(sums, 'dp_2', [(0, 1), (1, 0)])  1.15 us
    pallas_call x1, Pallas kernels, body(): pl.pallas_call(pick_kernel, out_shape=jax.ShapeDtypeStruct((n_dp, 32, LAN...  0.91 us
  transfers between devices with their start and end apart: 1, of which 1 were waited for; matrix products, arithmetic and copies ran while one was open for 0% of the time, Pallas kernels for 0%

profile of v5, /device:TPU:0, one launch (start us, length us, event | category | flops | bytes accessed | tf_op | source)
XLA Modules:
  0.0 42.2 jit_solution(13909616849877733509)
XLA Ops:
  0.6 0.0 copy-start
  0.6 0.0 copy-start.1
  0.7 0.0 copy-start.2
  0.7 0.9 %shard_map.59 = bf16[16,32,128]{2,1,0:T(8,128)(2,1)S(1)} custom-call(s32[3]{0:T(128)} %centers.1, bf16[4096,512]{1,0:T(8,128)(2,1)} %hid.3, bf16[16,4096]{1,0:T(8,128)(2,1)} %bitcast.9, s32[16,4096]{1,0:T(8,128)} %bitcast.7), custom_call_target="tpu_custom_call" | custom-call | tf_op jit(solution)/shard_map/pallas_call | solution.py:186
  1.6 12.1 %all_to_all.21.got = bf16[16,32,128]{2,1,0:T(8,128)(2,1)S(1)} all-to-all(bf16[16,32,128]{2,1,0:T(8,128)(2,1)S(1)} %shard_map.59), channel_id=1, replica_groups={{104,112,120,0,8,16,24,32,40,48,56,64,72,80,88,96},{105,113,121,1,9,17,..., dimensions={0} | all-to-all | bytes 262144 | tf_op jit(solution)/shard_map/all_to_all | solution.py:202
  13.7 0.0 copy-done
  13.7 0.0 copy-done.1
  13.7 0.0 copy-done.2
  13.7 1.9 %shard_map.60 = f32[8,8,640]{2,1,0:T(8,128)S(1)} custom-call(bf16[16,32,128]{2,1,0:T(8,128)(2,1)S(1)} %all_to_all.21.got, bf16[4096,512]{1,0:T(8,128)(2,1)S(1)} %copy-done, bf16[16,4096]{1,0:T(8,128)(2,1)S(1)} %bitcast.10, s32[16,4096]{1,0:T(8,128)S(1)} %bitcast.8), custom_call_target="tpu_custom_call" | custom-call | tf_op jit(solution)/shard_map/pallas_call | solution.py:204
  15.6 11.0 %all_to_all.22.parts = f32[8,8,640]{2,1,0:T(8,128)S(1)} all-to-all(f32[8,8,640]{2,1,0:T(8,128)S(1)} %shard_map.60), channel_id=1, replica_groups={{6,7,0,1,2,3,4,5},{14,15,8,9,10,11,12,13},{22,23,16,17,18,19,20,21},{30..., dimensions={0} | all-to-all | bytes 327680 | tf_op jit(solution)/shard_map/all_to_all | solution.py:216
  26.6 0.2 shard_map.61
  26.7 0.0 collective-permute-start
  26.8 1.2 %collective-permute-done.other = f32[8,128]{1,0:T(8,128)S(1)} collective-permute-done((f32[8,128]{1,0:T(8,128)S(1)}, f32[8,128]{1,0:T(8,128)S(1)}, u32[]{:S(2)}, u32[]{:S(2)}) %collective-permute-start) | collective-permute-done | bytes 4128 | tf_op jit(solution)/shard_map/ppermute | solution.py:228
  27.9 13.6 %all_to_all.23 = f32[64,1,128]{2,1,0:T(1,128)S(1)} all-to-all(f32[64,1,128]{2,1,0:T(1,128)S(1)} %bitcast.11), channel_id=1, replica_groups={{102,103,112,113,114,115,116,117,118,119,0,1,2,3,4,5,6,7,16,17,18,19,20..., dimensions={0} | all-to-all | bytes 65536 | tf_op jit(solution)/shard_map/all_to_all | solution.py:236
  41.6 0.6 %shard_map.63 = (f32[3]{0:T(128)}, f32[1,512]{1,0:T(1,128)}) custom-call(f32[64,128]{1,0:T(8,128)S(1)} %bitcast.12, f32[1,512]{1,0:T(1,128)S(1)} %get-tuple-element.7.mind), custom_call_target="tpu_custom_call" | custom-call | tf_op jit(solution)/shard_map/pallas_call | solution.py:237
  (1 shorter events, 0.0 us)
Async XLA Ops:
  0.6 13.0 %copy-start = (bf16[4096,512]{1,0:T(8,128)(2,1)S(1)}, bf16[4096,512]{1,0:T(8,128)(2,1)}, u32[]{:S(2)}) copy-start(bf16[4096,512]{1,0:T(8,128)(2,1)} %hid.3) | copy-start | bytes 12582916
  0.6 13.0 %copy-start.1 = (s32[4096,16]{0,1:T(8,128)S(1)}, s32[4096,16]{0,1:T(8,128)}, u32[]{:S(2)}) copy-start(s32[4096,16]{0,1:T(8,128)} %param.6) | copy-start | bytes 786436
  0.7 13.0 %copy-start.2 = (bf16[4096,16]{0,1:T(8,128)(2,1)S(1)}, bf16[4096,16]{0,1:T(8,128)(2,1)}, u32[]{:S(2)}) copy-start(bf16[4096,16]{0,1:T(8,128)(2,1)} %param.5) | copy-start | bytes 393220
  26.7 1.2 %collective-permute-start = (f32[8,128]{1,0:T(8,128)S(1)}, f32[8,128]{1,0:T(8,128)S(1)}, u32[]{:S(2)}, u32[]{:S(2)}) collective-permute-start(f32[8,128]{1,0:T(8,128)S(1)} %get-tuple-element.6.own), channel_id=1, source_target_pairs={{0,8},{8,0},{1,9},{9,1},{2,10},{10,2},{3,11},{11,3},{4,12},{12,4},... | collective-permute-start | bytes 12296 | tf_op jit(solution)/shard_map/ppermute | solution.py:228
